TPU v7x, 32 devices: a whole 2x2x4 slice. The times are simulated.
32 devices in a mesh: dp: 8 (over y, x, core), mp: 4 (over z).
Axes of the slice: x: 2, y: 2, z: 4, core: 2. Of those that a mesh axis runs over, the one named last changes fastest.
Arguments:
- grad_parts: bfloat16 [8, 4, 1024, 4096], P('dp', None, None, 'mp'), may hold values from -4000 to 4000
- master: float32 [4, 1024, 4096], P(None, 'dp', 'mp'), may hold values from -6 to 6
- first_moment: float32 [4, 1024, 4096], P(None, 'dp', 'mp'), may hold values from -4 to 4
- second_moment: float32 [4, 1024, 4096], P(None, 'dp', 'mp'), may hold values from 0.25 to 4
- left_basis: bfloat16 [4, 1024, 4096], P(None, 'dp', 'mp'), may hold values from -1 to 1, as said below
- right_basis: bfloat16 [4, 1024, 4096], P(None, 'dp', 'mp'), may hold values from -1 to 1, as said below
Outputs:
- weights: bfloat16 [4, 1024, 4096], P(None, None, 'mp')
- new_master: float32 [4, 1024, 4096], P(None, 'dp', 'mp')
- new_first: float32 [4, 1024, 4096], P(None, 'dp', 'mp')
- new_second: float32 [4, 1024, 4096], P(None, 'dp', 'mp')
Inputs may be any that keep to these rules, and one draw needn't show every extreme that they name: Each block left_basis[i, :, j * 1024 : (j + 1) * 1024] is an orthogonal 1024 x 1024 matrix up to rounding. Each block right_basis[i, :, j * 1024 : (j + 1) * 1024] is an orthogonal 1024 x 1024 matrix up to rounding.
All inputs are finite; a program needn't handle non-finite values.
Results may differ from a plain program's by a relative error of at most 0.02.
Values may be sent and summed in bfloat16 or wider, within the bound.
A program may use at most 128 MiB of HBM per device.

v0:
```python
import jax
import jax.numpy as jnp
from jax import lax
from jax.sharding import PartitionSpec as P

D = 4096
STEP = 10
beta_one = 0.95
beta_two = 0.95
epsilon = 1e-08
norm_epsilon = 1e-06
learning_rate = 0.3
decay_rate = 0.1


def per_device(grad_parts, master, first_moment, second_moment, left_basis, right_basis):
    gradient = lax.psum_scatter(grad_parts[0], "dp", scatter_dimension=1, tiled=True).astype(
        jnp.float32
    )
    squares_sum = lax.psum(jnp.sum(gradient * gradient), ("dp", "mp"))
    clip_scale = jnp.minimum(1.0, 2.0 * D / jnp.sqrt(squares_sum + norm_epsilon))
    grad_low = gradient.astype(jnp.bfloat16)
    right_full = lax.all_gather(right_basis, "dp", axis=1, tiled=True)
    turned = jnp.einsum(
        "isk,ikb->isb", grad_low, right_full, preferred_element_type=jnp.float32
    ).astype(jnp.bfloat16)
    left_cols = left_basis
    raw_term = jnp.einsum("isx,isb->xib", left_cols, turned, preferred_element_type=jnp.float32)
    rotated_rows = lax.psum_scatter(
        lax.optimization_barrier(raw_term.astype(jnp.bfloat16))
        .astype(jnp.float32)
        .astype(jnp.bfloat16),
        "dp",
        scatter_dimension=0,
        tiled=True,
    ).astype(jnp.float32)
    rotated = jnp.transpose(rotated_rows, (1, 0, 2))
    clipped = clip_scale * rotated
    new_first = beta_one * first_moment + (1.0 - beta_one) * clipped
    new_second = beta_two * second_moment + (1.0 - beta_two) * clipped * clipped
    bias_one = 1.0 - beta_one**STEP
    bias_two = 1.0 - beta_two**STEP
    direction = (new_first / bias_one / (jnp.sqrt(new_second / bias_two) + epsilon)).astype(
        jnp.bfloat16
    )
    back_rows = jnp.einsum(
        "isb,icb->isc", direction, right_full, preferred_element_type=jnp.float32
    ).astype(jnp.bfloat16)
    left_cols = left_basis
    update = jnp.einsum(
        "isk,ikc->isc",
        left_cols,
        lax.all_gather(back_rows, "dp", axis=1, tiled=True),
        preferred_element_type=jnp.float32,
    )
    new_master = master * (1.0 - learning_rate * decay_rate) - learning_rate * update
    weights = lax.all_gather(new_master.astype(jnp.bfloat16), "dp", axis=1, tiled=True)
    return (weights, new_master, new_first, new_second)


def solution(mesh):
    return jax.shard_map(
        per_device,
        mesh=mesh,
        in_specs=(
            P("dp", None, None, "mp"),
            P(None, "dp", "mp"),
            P(None, "dp", "mp"),
            P(None, "dp", "mp"),
            P(None, "dp", "mp"),
            P(None, "dp", "mp"),
        ),
        out_specs=(
            P(None, None, "mp"),
            P(None, "dp", "mp"),
            P(None, "dp", "mp"),
            P(None, "dp", "mp"),
        ),
        check_vma=False,
    )
```

profile of v0, /device:TPU:0, one launch (start us, length us, event | category | flops | bytes accessed | tf_op | source)
XLA Modules:
  0.0 386.3 jit_solution(4198887484840549487)
XLA Ops:
  7.2 0.0 copy-start
  7.2 0.0 reduce-scatter.5.cloned.1.call-start
  7.2 0.7 reduce-scatter.5.cloned.1.call-update
  7.9 0.0 all-gather.4.cloned.1.call-start
  8.0 0.7 all-gather.4.cloned.1.call-update
  8.7 0.0 reduce-scatter.7.cloned.1.call-start
  8.7 77.0 %reduce-scatter.5.cloned.1.call-done = bf16[4,128,1024]{2,1,0:T(8,128)(2,1)} async-done(((bf16[4,1024,1024]{2,1,0:T(8,128)(2,1)}), bf16[4,128,1024]{2,1,0:T(8,128)(2,1)}) %reduce-scatter.5.cloned.1.call-update) | async-done | bytes 1048592 | tf_op jit(solution)/shard_map/reduce_scatter | solution.py:17
  85.7 56.2 %all-gather.4.cloned.1.call-done = bf16[4,1024,1024]{2,1,0:T(8,128)(2,1)} async-done(((bf16[4,128,1024]{2,1,0:T(8,128)(2,1)}), bf16[4,1024,1024]{2,1,0:T(8,128)(2,1)}) %all-gather.4.cloned.1.call-update) | async-done | bytes 8388624 | tf_op jit(solution)/shard_map/all_gather | solution.py:23
  141.9 0.0 copy-done
  141.9 9.2 %convert_bitcast_fusion = bf16[1024,4,1024]{0,2,1:T(8,128)(2,1)} fusion(bf16[4,128,1024]{2,1,0:T(8,128)(2,1)S(1)} %copy-done, bf16[4,128,1024]{2,1,0:T(8,128)(2,1)} %reduce-scatter.5.cloned.1.call-done, bf16[4,1024,1024]{2,1,0:T(8,128)(2,1)} %all-gather.4.cloned.1.call-done), kind=kOutput, calls=%fused_computation | convolution fusion | flops 2152202240 | bytes 18874368 | tf_op jit(solution)/shard_map/isx,isb->xib/dot_general | solution.py:28
  151.1 11.8 %copy.26 = bf16[1024,4096]{1,0:T(8,128)(2,1)} copy(bf16[1024,4096]{0,1:T(8,128)(2,1)} %bitcast.17) | data formatting | bytes 16777216
  162.9 0.0 reduce-scatter.7.cloned.1.call-update
  162.9 0.0 all-gather.6.cloned.1.call-start
  162.9 1.9 copy.18
  164.8 2.4 multiply_reduce_fusion
  167.2 3.3 copy.19
  170.5 39.7 %psum.7 = f32[]{:T(128)} all-reduce(f32[]{:T(128)} %multiply_reduce_fusion), channel_id=1, replica_groups=mesh['dp'=8,'mp'=4] {'dp','mp'}, use_global_device_ids=true, to_apply=%region_2.0 | all-reduce | flops 1 | bytes 8 | tf_op jit(solution)/shard_map/psum | solution.py:20
  210.9 24.3 %reduce-scatter.7.cloned.1.call-done = bf16[128,4096]{1,0:T(8,128)(2,1)} async-done(((bf16[1024,4096]{1,0:T(8,128)(2,1)}), bf16[128,4096]{1,0:T(8,128)(2,1)}) %reduce-scatter.7.cloned.1.call-update) | async-done | bytes 1048592
  235.2 2.3 copy.27
  237.5 2.5 multiply_add_fusion
  239.9 0.0 copy-start.1
  240.0 0.0 copy-start.2
  240.0 1.3 copy-done.1
  241.3 0.7 copy-done.2
  242.0 0.0 copy-start.3
  242.0 7.0 %convolution_convert_fusion = bf16[4,128,1024]{1,2,0:T(8,128)(2,1)} fusion(bf16[4,1024,1024]{2,1,0:T(8,128)(2,1)} %all-gather.4.cloned.1.call-done, f32[4,128,1024]{1,2,0:T(8,128)S(1)} %get-tuple-element.13, f32[4,128,1024]{1,2,0:T(8,128)S(1)} %get-tuple-element.12), kind=kOutput, calls=%fused_computation.8 | convolution fusion | flops 1076887552 | bytes 13631488 | tf_op jit(solution)/shard_map/isb,icb->isc/dot_general | solution.py:46
  249.0 0.0 all-gather.6.cloned.1.call-update
  249.0 0.0 all-gather.8.cloned.1.call-start
  249.0 0.0 copy-done.3
  249.0 1.8 copy.17
  250.9 54.1 %all-gather.6.cloned.1.call-done = bf16[4,1024,1024]{1,2,0:T(8,128)(2,1)} async-done(((bf16[4,128,1024]{1,2,0:T(8,128)(2,1)}), bf16[4,1024,1024]{1,2,0:T(8,128)(2,1)}) %all-gather.6.cloned.1.call-update) | async-done | bytes 8388624 | tf_op jit(solution)/shard_map/all_gather | solution.py:53
  305.0 7.4 %fusion.5 = (bf16[4,128,1024]{1,2,0:T(8,128)(2,1)}, f32[4,128,1024]{1,2,0:T(8,128)S(1)}) fusion(bf16[4,1024,1024]{1,2,0:T(8,128)(2,1)} %all-gather.6.cloned.1.call-done, bf16[4,128,1024]{2,1,0:T(8,128)(2,1)S(1)} %copy-done, f32[4,128,1024]{1,2,0:T(8,128)} %copy.17), kind=kOutput, calls=%fused_computation.14 | convolution fusion | flops 1075838976 | bytes 14680064 | tf_op jit(solution)/shard_map/isk,ikc->isc/dot_general | solution.py:50
  312.4 0.0 all-gather.8.cloned.1.call-update
  312.4 2.9 copy.22
  315.3 2.9 copy.23
  318.2 1.8 copy.21
  320.0 48.4 %all-gather.8.cloned.1.call-done = bf16[4,1024,1024]{1,2,0:T(8,128)(2,1)} async-done(((bf16[4,128,1024]{1,2,0:T(8,128)(2,1)}), bf16[4,1024,1024]{1,2,0:T(8,128)(2,1)}) %all-gather.8.cloned.1.call-update) | async-done | bytes 8388624 | tf_op jit(solution)/shard_map/all_gather | solution.py:57
  368.4 11.3 %copy.20 = bf16[4,1024,1024]{2,1,0:T(8,128)(2,1)} copy(bf16[4,1024,1024]{1,2,0:T(8,128)(2,1)} %all-gather.8.cloned.1.call-done) | data formatting | bytes 16777216
Async XLA Ops:
  7.2 134.7 %copy-start = (bf16[4,128,1024]{2,1,0:T(8,128)(2,1)S(1)}, bf16[4,128,1024]{2,1,0:T(8,128)(2,1)}, u32[]{:S(2)}) copy-start(bf16[4,128,1024]{2,1,0:T(8,128)(2,1)} %param.10) | copy-start | bytes 3145732
  7.2 78.5 %reduce-scatter.5.cloned.1.call-start = ((), (), s32[]{:S(2)}) async-start(), calls=%async_computation.2 | async-start | bytes 9437184 | tf_op jit(solution)/shard_map/reduce_scatter | solution.py:17
  7.9 134.0 %all-gather.4.cloned.1.call-start = ((), (), s32[]{:S(2)}) async-start(), calls=%async_computation.3 | async-start | bytes 9437184 | tf_op jit(solution)/shard_map/all_gather | solution.py:23
  8.7 226.6 %reduce-scatter.7.cloned.1.call-start = ((), (), s32[]{:S(2)}) async-start(), calls=%async_computation.6 | async-start | bytes 9437184
  162.9 142.1 %all-gather.6.cloned.1.call-start = ((), (), s32[]{:S(2)}) async-start(), calls=%async_computation.4 | async-start | bytes 9437184 | tf_op jit(solution)/shard_map/all_gather | solution.py:53
  239.9 1.3 copy-start.1
  240.0 2.0 copy-start.2
  242.0 7.1 %copy-start.3 = (f32[4,128,1024]{2,1,0:T(8,128)S(1)}, f32[4,128,1024]{2,1,0:T(8,128)}, u32[]{:S(2)}) copy-start(f32[4,128,1024]{2,1,0:T(8,128)} %param.7) | copy-start | bytes 6291460
  249.0 119.5 %all-gather.8.cloned.1.call-start = ((), (), s32[]{:S(2)}) async-start(), calls=%async_computation.5 | async-start | bytes 9437184 | tf_op jit(solution)/shard_map/all_gather | solution.py:57
Sparse Core Ops, SparseCore 0:
  11.4 74.2 reduce-scatter.4
  87.6 54.2 all-gather.3
  163.0 72.1 reduce-scatter.6
  249.1 55.8 all-gather.5
  312.5 55.8 all-gather.7
where the time goes:
time: 387 us; the launch traced here: 386 us
  waiting for transfers between devices  262 us (68%)
  local copies, waits for them, and re-layouts  41.9 us (11%)
  blocking collectives  39.7 us (10%)
  matrix products  23.6 us (6%)
  between operations  14.5 us (4%)
  other arithmetic  4.83 us (1%)
    reduce_scatter x1, waiting for transfers between devices, per_device(): lax.psum_scatter(grad_parts[0], 'dp', scatter_dimension=1, tiled=True)  77 us
    all_gather x1, waiting for transfers between devices, per_device(): right_full = lax.all_gather(right_basis, 'dp', axis=1, tiled=True)  56.2 us
    all_gather x1, waiting for transfers between devices, per_device(): lax.all_gather(back_rows, 'dp', axis=1, tiled=True)  54.1 us
    all_gather x1, waiting for transfers between devices, per_device(): lax.all_gather(new_master.astype(jnp.bfloat16), 'dp', axis=1, tiled=True)  48.4 us
    unnamed x17, local copies, waits for them, and re-layouts  41.9 us
    psum x1, blocking collectives, per_device(): squares_sum = lax.psum(jnp.sum(gradient * gradient), ('dp', 'mp'))  39.7 us
    unnamed x6, waiting for transfers between devices  25.7 us
    dot_general x1, matrix products, per_device(): jnp.einsum('isx,isb->xib', left_cols, turned, preferred_element_type=jnp....  9.19 us
  transfers between devices with their start and end apart: 5, of which 5 were waited for; matrix products, arithmetic and copies ran while one was open for 4% of the time, Pallas kernels for 0%

commit v1 on v0

--- a/solution.py
+++ b/solution.py
@@ -47,12 +47,38 @@
         "isb,icb->isc", direction, right_full, preferred_element_type=jnp.float32
     ).astype(jnp.bfloat16)
     left_cols = left_basis
-    update = jnp.einsum(
+    size, index, rows = (lax.axis_size("dp"), lax.axis_index("dp"), back_rows.shape[1])
+    right = [(i, (i + 1) % size) for i in range(size)]
+    downward = [(i, (i - 1) % size) for i in range(size)]
+    half = size // 2
+    from_left = from_right = back_rows
+    subtotal = jnp.einsum(
         "isk,ikc->isc",
-        left_cols,
-        lax.all_gather(back_rows, "dp", axis=1, tiled=True),
+        lax.dynamic_slice_in_dim(left_cols, index * rows, back_rows.shape[1], axis=2),
+        back_rows,
         preferred_element_type=jnp.float32,
     )
+    for lap in range(1, half + 1):
+        from_left = lax.ppermute(from_left, "dp", right)
+        if lap < size - half:
+            from_right = lax.ppermute(from_right, "dp", downward)
+            subtotal = subtotal + jnp.einsum(
+                "isk,ikc->isc",
+                lax.dynamic_slice_in_dim(
+                    left_cols, (index + lap) % size * rows, from_right.shape[1], axis=2
+                ),
+                from_right,
+                preferred_element_type=jnp.float32,
+            )
+        subtotal = subtotal + jnp.einsum(
+            "isk,ikc->isc",
+            lax.dynamic_slice_in_dim(
+                left_cols, (index - lap) % size * rows, from_left.shape[1], axis=2
+            ),
+            from_left,
+            preferred_element_type=jnp.float32,
+        )
+    update = subtotal
     new_master = master * (1.0 - learning_rate * decay_rate) - learning_rate * update
     weights = lax.all_gather(new_master.astype(jnp.bfloat16), "dp", axis=1, tiled=True)
     return (weights, new_master, new_first, new_second)

time: 387 us -> 413 us (1.067)
  waiting for transfers between devices: 262 us -> 285 us
  local copies, waits for them, and re-layouts: 41.9 us -> 33.9 us
  starting transfers between devices: 0.2 us -> 6.34 us
  matrix products: 23.6 us -> 28.6 us
    ppermute x0 -> x7, waiting for transfers between devices: none -> 76.1 us  [the longest x4 76.1 us: per_device(): from_left = lax.ppermute(from_left, 'dp', right)]
    all_gather x1 -> x0, waiting for transfers between devices: 54.1 us -> none  [per_device(): lax.all_gather(back_rows, 'dp', axis=1, tiled=True)]
    unnamed x17 -> x21, local copies, waits for them, and re-layouts: 41.9 us -> 33.9 us
    ppermute x0 -> x7, starting transfers between devices: none -> 6.18 us  [the longest x3 6.12 us: per_device(): from_right = lax.ppermute(from_right, 'dp', downward)]
    dot_general x1 -> x8, matrix products: 7.4 us -> 11.9 us  [the longest x4 6.49 us: per_device(): jnp.einsum('isk,ikc->isc', lax.dynamic_slice_in_dim(left_cols, (index - l...]
    unnamed x6 -> x5, waiting for transfers between devices: 25.7 us -> 26 us
  transfers between devices with their start and end apart: 5 -> 11, of which waited for: 5 -> 8; matrix products, arithmetic and copies ran while one was open for 4% -> 5% of each run, Pallas kernels for 0% -> 0%
where the time goes in v1:
time: 413 us; the launch traced here: 412 us
  waiting for transfers between devices  285 us (69%)
  blocking collectives  39.9 us (10%)
  local copies, waits for them, and re-layouts  33.9 us (8%)
  matrix products  28.6 us (7%)
  between operations  14.6 us (4%)
  starting transfers between devices  6.34 us (2%)
  other arithmetic  4.22 us (1%)
    reduce_scatter x1, waiting for transfers between devices, per_device(): lax.psum_scatter(grad_parts[0], 'dp', scatter_dimension=1, tiled=True)  77 us
    ppermute x4, waiting for transfers between devices, per_device(): from_left = lax.ppermute(from_left, 'dp', right)  76.1 us
    all_gather x1, waiting for transfers between devices, per_device(): right_full = lax.all_gather(right_basis, 'dp', axis=1, tiled=True)  56.2 us
    all_gather x1, waiting for transfers between devices, per_device(): lax.all_gather(new_master.astype(jnp.bfloat16), 'dp', axis=1, tiled=True)  49.5 us
    psum x1, blocking collectives, per_device(): squares_sum = lax.psum(jnp.sum(gradient * gradient), ('dp', 'mp'))  39.9 us
    unnamed x21, local copies, waits for them, and re-layouts  33.9 us
    unnamed x5, waiting for transfers between devices  26 us
    dot_general x1, matrix products, per_device(): jnp.einsum('isx,isb->xib', left_cols, turned, preferred_element_type=jnp....  9.19 us
  transfers between devices with their start and end apart: 11, of which 8 were waited for; matrix products, arithmetic and copies ran while one was open for 5% of the time, Pallas kernels for 0%

profile of v1, /device:TPU:0, one launch (start us, length us, event | category | flops | bytes accessed | tf_op | source)
XLA Modules:
  0.0 412.3 jit_solution(14110599128187330156)
XLA Ops:
  7.2 0.0 copy-start
  7.2 0.0 reduce-scatter.5.cloned.1.call-start
  7.2 0.7 reduce-scatter.5.cloned.1.call-update
  7.9 0.0 all-gather.3.cloned.1.call-start
  8.0 0.7 all-gather.3.cloned.1.call-update
  8.7 0.0 reduce-scatter.7.cloned.1.call-start
  8.7 77.0 %reduce-scatter.5.cloned.1.call-done = bf16[4,128,1024]{2,1,0:T(8,128)(2,1)} async-done(((bf16[4,1024,1024]{2,1,0:T(8,128)(2,1)}), bf16[4,128,1024]{2,1,0:T(8,128)(2,1)}) %reduce-scatter.5.cloned.1.call-update) | async-done | bytes 1048592 | tf_op jit(solution)/shard_map/reduce_scatter | solution.py:17
  85.7 56.2 %all-gather.3.cloned.1.call-done = bf16[4,1024,1024]{2,1,0:T(8,128)(2,1)} async-done(((bf16[4,128,1024]{2,1,0:T(8,128)(2,1)}), bf16[4,1024,1024]{2,1,0:T(8,128)(2,1)}) %all-gather.3.cloned.1.call-update) | async-done | bytes 8388624 | tf_op jit(solution)/shard_map/all_gather | solution.py:23
  141.9 9.2 %convert_bitcast_fusion = bf16[1024,4,1024]{0,2,1:T(8,128)(2,1)} fusion(bf16[4,128,1024]{2,1,0:T(8,128)(2,1)S(1)} %copy-done, bf16[4,128,1024]{2,1,0:T(8,128)(2,1)} %reduce-scatter.5.cloned.1.call-done, bf16[4,1024,1024]{2,1,0:T(8,128)(2,1)} %all-gather.3.cloned.1.call-done), kind=kOutput, calls=%fused_computation | convolution fusion | flops 2152202240 | bytes 18874368 | tf_op jit(solution)/shard_map/isx,isb->xib/dot_general | solution.py:28
  151.1 11.3 %copy.23 = bf16[1024,4096]{1,0:T(8,128)(2,1)} copy(bf16[1024,4096]{0,1:T(8,128)(2,1)} %bitcast.21) | data formatting | bytes 16777216
  162.4 0.0 reduce-scatter.7.cloned.1.call-update
  162.4 0.0 all-gather.5.cloned.1.call-start
  162.5 3.0 copy.15
  165.4 1.1 multiply_reduce_fusion
  166.6 3.1 copy.16
  169.6 39.9 %psum.7 = f32[]{:T(128)} all-reduce(f32[]{:T(128)} %multiply_reduce_fusion), channel_id=1, replica_groups=mesh['dp'=8,'mp'=4] {'dp','mp'}, use_global_device_ids=true, to_apply=%region_2.0 | all-reduce | flops 1 | bytes 8 | tf_op jit(solution)/shard_map/psum | solution.py:20
  210.2 24.6 %reduce-scatter.7.cloned.1.call-done = bf16[128,4096]{1,0:T(8,128)(2,1)} async-done(((bf16[1024,4096]{1,0:T(8,128)(2,1)}), bf16[128,4096]{1,0:T(8,128)(2,1)}) %reduce-scatter.7.cloned.1.call-update) | async-done | bytes 1048592
  234.8 2.3 copy.24
  237.0 3.1 multiply_add_fusion
  240.1 0.0 copy-start.1
  240.1 7.5 %convolution_convert_fusion = bf16[4,128,1024]{2,1,0:T(8,128)(2,1)S(1)} fusion(bf16[4,1024,1024]{2,1,0:T(8,128)(2,1)} %all-gather.3.cloned.1.call-done, f32[4,128,1024]{1,2,0:T(8,128)S(1)} %get-tuple-element.13, f32[4,128,1024]{1,2,0:T(8,128)S(1)} %get-tuple-element.12), kind=kOutput, calls=%fused_computation.8 | convolution fusion | flops 1076887552 | bytes 13631488 | tf_op jit(solution)/shard_map/isb,icb->isc/dot_general | solution.py:46
  247.6 0.0 copy-start.4
  247.6 0.1 collective-permute-start.1
  247.7 0.9 copy-done.4
  248.6 1.7 collective-permute-start
  250.3 22.8 %collective-permute-done.1 = bf16[4,128,1024]{2,1,0:T(8,128)(2,1)S(1)} collective-permute-done((bf16[4,128,1024]{2,1,0:T(8,128)(2,1)S(1)}, bf16[4,128,1024]{2,1,0:T(8,128)(2,1)S(1)}, u32[]{:S(2)}, u32[]{:S(2)}) %collective-permute-start.1) | collective-permute-done | bytes 1048608 | tf_op jit(solution)/shard_map/ppermute | solution.py:62
  273.1 0.0 collective-permute-start.3
  273.1 1.0 copy-done.5
  274.1 1.7 collective-permute-start.2
  275.8 23.3 %collective-permute-done.3 = bf16[4,128,1024]{2,1,0:T(8,128)(2,1)} collective-permute-done((bf16[4,128,1024]{2,1,0:T(8,128)(2,1)S(1)}, bf16[4,128,1024]{2,1,0:T(8,128)(2,1)}, u32[]{:S(2)}, u32[]{:S(2)}) %collective-permute-start.3) | collective-permute-done | bytes 1048608 | tf_op jit(solution)/shard_map/ppermute | solution.py:62
  299.1 1.7 fusion.16
  300.9 0.4 fusion.12
  301.3 2.7 collective-permute-start.4
  304.0 1.6 fusion.14
  305.7 20.0 %collective-permute-done.5 = bf16[4,128,1024]{2,1,0:T(8,128)(2,1)} collective-permute-done((bf16[4,128,1024]{2,1,0:T(8,128)(2,1)}, bf16[4,128,1024]{2,1,0:T(8,128)(2,1)}, u32[]{:S(2)}, u32[]{:S(2)}) %collective-permute-start.5) | collective-permute-done | bytes 1048608 | tf_op jit(solution)/shard_map/ppermute | solution.py:62
  325.7 0.0 collective-permute-start.6
  325.7 1.6 fusion.8
  327.3 1.7 fusion.10
  329.0 1.7 fusion.4
  330.6 0.0 copy-start.3
  330.7 0.4 fusion.6
  331.1 9.9 %collective-permute-done.6 = bf16[4,128,1024]{2,1,0:T(8,128)(2,1)S(1)} collective-permute-done((bf16[4,128,1024]{2,1,0:T(8,128)(2,1)}, bf16[4,128,1024]{2,1,0:T(8,128)(2,1)S(1)}, u32[]{:S(2)}, u32[]{:S(2)}) %collective-permute-start.6) | collective-permute-done | bytes 1048608 | tf_op jit(solution)/shard_map/ppermute | solution.py:62
  341.0 2.8 fusion.28
  343.8 0.0 all-gather.5.cloned.1.call-update
  343.8 2.9 copy.18
  346.7 1.8 copy.19
  348.5 49.5 %all-gather.5.cloned.1.call-done = bf16[4,1024,1024]{2,1,0:T(8,128)(2,1)} async-done(((bf16[4,128,1024]{2,1,0:T(8,128)(2,1)}), bf16[4,1024,1024]{2,1,0:T(8,128)(2,1)}) %all-gather.5.cloned.1.call-update) | async-done | bytes 8388624 | tf_op jit(solution)/shard_map/all_gather | solution.py:83
  398.0 7.8 %copy.26 = bf16[4,1024,1024]{2,1,0:T(8,128)(2,1)} copy(bf16[4,1024,1024]{2,1,0:T(8,128)(2,1)} %all-gather.5.cloned.1.call-done) | data formatting | bytes 16777216
  (12 shorter events, 0.0 us)
Async XLA Ops:
  7.2 134.7 %copy-start = (bf16[4,128,1024]{2,1,0:T(8,128)(2,1)S(1)}, bf16[4,128,1024]{2,1,0:T(8,128)(2,1)}, u32[]{:S(2)}) copy-start(bf16[4,128,1024]{2,1,0:T(8,128)(2,1)} %param.10) | copy-start | bytes 3145732
  7.2 78.5 %reduce-scatter.5.cloned.1.call-start = ((), (), s32[]{:S(2)}) async-start(), calls=%async_computation.2 | async-start | bytes 9437184 | tf_op jit(solution)/shard_map/reduce_scatter | solution.py:17
  7.9 134.0 %all-gather.3.cloned.1.call-start = ((), (), s32[]{:S(2)}) async-start(), calls=%async_computation.3 | async-start | bytes 9437184 | tf_op jit(solution)/shard_map/all_gather | solution.py:23
  8.7 226.1 %reduce-scatter.7.cloned.1.call-start = ((), (), s32[]{:S(2)}) async-start(), calls=%async_computation.5 | async-start | bytes 9437184
  162.4 3.0 copy-start.2
  162.4 235.6 %all-gather.5.cloned.1.call-start = ((), (), s32[]{:S(2)}) async-start(), calls=%async_computation.4 | async-start | bytes 9437184 | tf_op jit(solution)/shard_map/all_gather | solution.py:83
  240.1 7.5 %copy-start.1 = (f32[4,128,1024]{1,2,0:T(8,128)}, f32[4,128,1024]{1,2,0:T(8,128)S(1)}, u32[]{:S(2)}) copy-start(f32[4,128,1024]{1,2,0:T(8,128)S(1)} %get-tuple-element.12) | copy-start | bytes 6291460
  247.6 1.0 copy-start.4
  247.6 25.5 %collective-permute-start.1 = (bf16[4,128,1024]{2,1,0:T(8,128)(2,1)S(1)}, bf16[4,128,1024]{2,1,0:T(8,128)(2,1)S(1)}, u32[]{:S(2)}, u32[]{:S(2)}) collective-permute-start(bf16[4,128,1024]{2,1,0:T(8,128)(2,1)S(1)} %convolution_convert_fusion), channel_id=1, source_target_pairs={{0,4},{4,8},{8,12},{12,16},{16,20},{20,24},{24,28},{28,0},{1,5},{5... | collective-permute-start | bytes 3145736 | tf_op jit(solution)/shard_map/ppermute | solution.py:62
  248.6 24.6 %collective-permute-start = (bf16[4,128,1024]{2,1,0:T(8,128)(2,1)S(1)}, bf16[4,128,1024]{2,1,0:T(8,128)(2,1)}, u32[]{:S(2)}, u32[]{:S(2)}) collective-permute-start(bf16[4,128,1024]{2,1,0:T(8,128)(2,1)S(1)} %convolution_convert_fusion), channel_id=1, source_target_pairs={{0,28},{4,0},{8,4},{12,8},{16,12},{20,16},{24,20},{28,24},{1,29},{... | collective-permute-start | bytes 3145736 | tf_op jit(solution)/shard_map/ppermute | solution.py:64
  273.1 1.0 copy-start.5
  273.1 26.0 %collective-permute-start.3 = (bf16[4,128,1024]{2,1,0:T(8,128)(2,1)S(1)}, bf16[4,128,1024]{2,1,0:T(8,128)(2,1)}, u32[]{:S(2)}, u32[]{:S(2)}) collective-permute-start(bf16[4,128,1024]{2,1,0:T(8,128)(2,1)S(1)} %collective-permute-done.1), channel_id=1, source_target_pairs={{0,4},{4,8},{8,12},{12,16},{16,20},{20,24},{24,28},{28,0},{1,5},{5... | collective-permute-start | bytes 3145736 | tf_op jit(solution)/shard_map/ppermute | solution.py:62
  274.1 27.2 %collective-permute-start.2 = (bf16[4,128,1024]{2,1,0:T(8,128)(2,1)}, bf16[4,128,1024]{2,1,0:T(8,128)(2,1)}, u32[]{:S(2)}, u32[]{:S(2)}) collective-permute-start(bf16[4,128,1024]{2,1,0:T(8,128)(2,1)} %collective-permute-done), channel_id=1, source_target_pairs={{0,28},{4,0},{8,4},{12,8},{16,12},{20,16},{24,20},{28,24},{1,29},{... | collective-permute-start | bytes 3145736 | tf_op jit(solution)/shard_map/ppermute | solution.py:64
  299.1 26.5 %collective-permute-start.5 = (bf16[4,128,1024]{2,1,0:T(8,128)(2,1)}, bf16[4,128,1024]{2,1,0:T(8,128)(2,1)}, u32[]{:S(2)}, u32[]{:S(2)}) collective-permute-start(bf16[4,128,1024]{2,1,0:T(8,128)(2,1)} %collective-permute-done.3), channel_id=1, source_target_pairs={{0,4},{4,8},{8,12},{12,16},{16,20},{20,24},{24,28},{28,0},{1,5},{5... | collective-permute-start | bytes 3145736 | tf_op jit(solution)/shard_map/ppermute | solution.py:62
  299.1 1.7 copy-start.6
  301.3 29.3 %collective-permute-start.4 = (bf16[4,128,1024]{2,1,0:T(8,128)(2,1)}, bf16[4,128,1024]{2,1,0:T(8,128)(2,1)S(1)}, u32[]{:S(2)}, u32[]{:S(2)}) collective-permute-start(bf16[4,128,1024]{2,1,0:T(8,128)(2,1)} %collective-permute-done.2), channel_id=1, source_target_pairs={{0,28},{4,0},{8,4},{12,8},{16,12},{20,16},{24,20},{28,24},{1,29},{... | collective-permute-start | bytes 3145736 | tf_op jit(solution)/shard_map/ppermute | solution.py:64
  325.7 15.3 %collective-permute-start.6 = (bf16[4,128,1024]{2,1,0:T(8,128)(2,1)}, bf16[4,128,1024]{2,1,0:T(8,128)(2,1)S(1)}, u32[]{:S(2)}, u32[]{:S(2)}) collective-permute-start(bf16[4,128,1024]{2,1,0:T(8,128)(2,1)} %collective-permute-done.5), channel_id=1, source_target_pairs={{0,4},{4,8},{8,12},{12,16},{16,20},{20,24},{24,28},{28,0},{1,5},{5... | collective-permute-start | bytes 3145736 | tf_op jit(solution)/shard_map/ppermute | solution.py:62
  330.6 10.4 %copy-start.3 = (f32[4,128,1024]{2,1,0:T(8,128)S(1)}, f32[4,128,1024]{2,1,0:T(8,128)}, u32[]{:S(2)}) copy-start(f32[4,128,1024]{2,1,0:T(8,128)} %param.7) | copy-start | bytes 6291460
Sparse Core Ops, SparseCore 0:
  11.4 74.2 reduce-scatter.4
  87.6 54.2 all-gather.2
  162.5 72.1 reduce-scatter.6
  343.9 54.0 all-gather.4
